TPU v7x, 32 devices: a whole 2x2x4 slice. The times are simulated.
32 devices in a mesh: row: 16 (over z, x, core), col: 2 (over y).
Axes of the slice: x: 2, y: 2, z: 4, core: 2. Of those that a mesh axis runs over, the one named last changes fastest.
Arguments:
- particles: bfloat16 [64, 64, 4096], P(('row', 'col')), may hold values from -6 to 6
- orientation: int32 [64], P(('row', 'col')), may hold values from 0 to 23
- tilt: int32 [64], P(('row', 'col')), may hold values from 0 to 7
- weight: float32 [64], P(('row', 'col')), may hold values from 0.3 to 3
Outputs:
- reference_map: float32 [2, 64, 4096], P(None, 'row', 'col')
Inputs may be any that keep to these rules, and one draw needn't show every extreme that they name: `orientation`: an index into the table of 24 rotations. `tilt`: an index into the 8 tilt ranges.
All inputs are finite; a program needn't handle non-finite values.
Results may differ from a plain program's by a relative error of at most 0.0054.
Values sent between devices are 32-bit elements; how exact they have to be, the bound alone decides.
A program may use at most 64 MiB of HBM per device.

v0:
```python
import math

import jax
import jax.numpy as jnp
import numpy as np
from jax import lax
from jax.experimental import pallas as pl
from jax.experimental.pallas import tpu as pltpu
from jax.sharding import PartitionSpec as P

TILTS = 8
BEAM_LIST = (0, 0, 1, 2, 1, 2)
ACROSS_LIST = (2, 1, 2, 1, 0, 0)
wiener_offset = 1.0
MESH = pl.DeviceIdType.MESH
PAD = 8
BLOCKS = 8


def tables(width):
    index = np.arange(width)
    angle = (index[:, None] * index[None, :] % width).astype(np.float32) * np.float32(2.0 * math.pi / width)
    factor = np.float32(1.0 / math.sqrt(width))
    lefts, turns, rights, rows = [], [], [], []
    for reverse in (False, True):
        c, s = np.cos(angle) * factor, np.sin(angle) * factor
        if reverse:
            c, s = c[:, ::-1], s[:, ::-1]
        zero = np.zeros_like(c)
        lefts.append(np.concatenate([c, -s], 0))
        turns.append(np.block([[c, zero], [-s, zero], [zero, c], [zero, -s]]))
        plain, turned, blank = np.concatenate([c.T, -s.T], 1), np.concatenate([s.T, c.T], 1), np.zeros((width, 2 * width))
        rights.append(np.block([[plain, blank], [blank, plain], [turned, blank], [blank, turned]]))
        rows.append(np.concatenate([c, s], 1))
    return [jnp.asarray(np.stack(t), jnp.float32).astype(jnp.bfloat16) for t in (lefts, turns, rights, rows)]


def frequency(index, width):
    return jnp.abs(jnp.where(index < width // 2, index, index - width))


def transform_kernel(
    width, ori, tilt, weight, x_ref, left_ref, turn_ref, right_ref, row_ref, held, rows_out, par_ref, cls_ref, loose, cube
):
    p = pl.program_id(0)
    wide = 2 * width
    half = width // 2
    step = width + PAD
    orient = ori[p]
    perm = orient // 4
    flip_z = orient % 2
    flip_y = orient // 2 % 2
    parity = jnp.where((perm == 1) | (perm == 2) | (perm == 5), 1, 0)
    flip_x = (flip_z + flip_y + parity) % 2
    swapped = (perm == 1) | (perm == 4) | (perm == 5)
    whole = (perm == 0) | (perm == 5)
    outer = (perm == 2) | (perm == 4)
    scale = weight[p]

    @pl.when(p == 0)
    def _():
        cls_ref[...] = jnp.zeros_like(cls_ref)

    label = lax.broadcasted_iota(jnp.int32, cls_ref.shape, 1)
    cls_ref[...] += jnp.where(label == perm * TILTS + tilt[p], scale, 0.0)

    slope = (5 + 2 * tilt[p]).astype(jnp.float32)
    line = lax.broadcasted_iota(jnp.int32, (8, wide), 0)
    par = jnp.where(line == 3, scale, 0.0)
    for perm_index in range(6):
        here = (line == BEAM_LIST[perm_index]) & (perm == perm_index)
        there = (line == ACROSS_LIST[perm_index]) & (perm == perm_index)
        par = par + jnp.where(here, 4.0, 0.0) - jnp.where(there, slope, 0.0)
    par_ref[p] = par

    flip_sub = jnp.where(whole, flip_z, flip_y)
    flip_lane = jnp.where(whole | outer, flip_x, flip_z)
    flip_last = jnp.where(whole, flip_y, jnp.where(outer, flip_z, flip_x))
    rows_out[p] = row_ref[flip_last]
    blocks = width // 2
    left = lax.broadcasted_iota(jnp.int32, (half, wide), 1) < width

    def gather():
        for i in range(half):
            cube[:, i * wide : (i + 1) * wide] = loose[i * step : i * step + width, :].astype(jnp.bfloat16)

    @pl.when(whole)
    def _():
        cube[...] = x_ref[0]

    @pl.when(outer)
    def _():
        for b in range(blocks):
            part = x_ref[0, :, b * wide : (b + 1) * wide].astype(jnp.float32)
            top, low = part[:half], part[half:]
            loose[pl.ds(2 * b, half, stride=step), :] = jnp.where(left, top, pltpu.roll(low, width, 1))
            loose[pl.ds(2 * b + 1, half, stride=step), :] = jnp.where(left, pltpu.roll(top, width, 1), low)
        gather()

    @pl.when(jnp.logical_not(whole | outer))
    def _():
        for b in range(blocks):
            part = x_ref[0, :, b * wide : (b + 1) * wide].astype(jnp.float32).T
            for h in range(2):
                top, low = part[h * width : h * width + half], part[h * width + half : (h + 1) * width]
                loose[pl.ds(2 * b + h, half, stride=step), :] = jnp.concatenate([top, low], 1)
        gather()

    def place(b, h):
        return jnp.where(whole, 2 * b + h, b + h * half)

    def put(b, h, value):
        held[p, pl.ds(place(b, h), width, stride=step), :] = value

    @pl.when(jnp.logical_not(swapped))
    def _():
        first, second = left_ref[flip_sub], right_ref[flip_lane]
        for base in range(0, blocks, BLOCKS):
            out = jnp.dot(first, cube[:, base * wide : (base + BLOCKS) * wide], preferred_element_type=jnp.float32)
            tall = jnp.concatenate(
                [
                    jnp.concatenate([out[:width, u * wide : (u + 1) * wide], out[width:, u * wide : (u + 1) * wide]], 1)
                    for u in range(BLOCKS)
                ],
                0,
            ).astype(jnp.bfloat16)
            done = jnp.dot(tall, second, preferred_element_type=jnp.float32)
            for u in range(BLOCKS):
                part = done[u * width : (u + 1) * width]
                put(base + u, 0, part[:, :wide])
                put(base + u, 1, part[:, wide:])

    @pl.when(swapped)
    def _():
        first, second = turn_ref[flip_lane], right_ref[flip_sub]
        for base in range(0, blocks, BLOCKS):
            stack = jnp.concatenate([cube[:, b * wide : (b + 1) * wide] for b in range(base, base + BLOCKS)], 0)
            out = lax.dot_general(first, stack, (((1,), (1,)), ((), ())), preferred_element_type=jnp.float32)
            tall = []
            for u in range(0, BLOCKS, 2):
                for h in range(2):
                    part = out[h * wide : (h + 1) * wide, u * width : (u + 2) * width]
                    tall.append(jnp.concatenate([part[:width], part[width:]], 1))
            tall = jnp.concatenate(tall, 0).astype(jnp.bfloat16)
            done = jnp.dot(tall, second, preferred_element_type=jnp.float32)
            for u in range(0, BLOCKS, 2):
                for h in range(2):
                    part = done[(u + h) * width : (u + h + 1) * width]
                    put(base + u, h, part[:, :wide])
                    put(base + u + 1, h, part[:, wide:])


def transform(particles, orientation, tilt, weight):
    count, width, area = particles.shape
    step = width + PAD
    wide = 2 * width
    consts = tables(width)
    smem = pl.BlockSpec(memory_space=pltpu.SMEM)
    vmem = pl.BlockSpec(memory_space=pltpu.VMEM)
    whole = [pl.BlockSpec(t.shape, lambda i: (0, 0, 0)) for t in consts]
    return pl.pallas_call(
        lambda *refs: transform_kernel(width, *refs),
        grid=(count,),
        in_specs=[smem, smem, smem, pl.BlockSpec((1, width, area), lambda i: (i, 0, 0))] + whole,
        out_specs=[vmem] * 4,
        out_shape=[
            pltpu.VMEM((count, width * step, wide), jnp.float32),
            pltpu.VMEM((count, width, wide), jnp.bfloat16),
            pltpu.VMEM((count, 8, wide), jnp.float32),
            pltpu.VMEM((8, 128), jnp.float32),
        ],
        scratch_shapes=[
            pltpu.VMEM((width // 2 * step, wide), jnp.float32),
            pltpu.VMEM((width, area), jnp.bfloat16),
        ],
        compiler_params=pltpu.CompilerParams(vmem_limit_bytes=32 << 20),
        name="transform",
    )(orientation, tilt, weight, particles, *consts)


def exchange_kernel(
    n_z, n_col, width, held, table, par, cls, fin, acc, slant, got1, sum1, got2, sum2, got3,
    zgot, zsum, ygot, cgot1, csum1, cgot2, csum2, cgot3, s1, r1, s2, r2, s3, r3, cs1, cr1, cs2, cr2, cs3, cr3, sz, rz, sy, ry,
):
    row, col = lax.axis_index("row"), lax.axis_index("col")
    z, x, core = row // 4, row // 2 % 2, row % 2
    band = width // n_col
    group = 2 * n_col
    member = x * n_col + col
    pair = (row + 1 - 2 * core, col)

    def mate(k):
        m = lax.rem(member + k, group)
        return m, (z * 4 + m // n_col * 2 + core, lax.rem(m, n_col))

    def far(k):
        t = lax.rem(z + k, n_z)
        return t, (t * 4 + x * 2 + core, col)

    def send(src, dst, ssem, rsem, to):
        copy = pltpu.make_async_remote_copy(
            src_ref=src, dst_ref=dst, send_sem=ssem, recv_sem=rsem, device_id=to, device_id_type=MESH
        )
        copy.start()
        return copy

    count = held.shape[0]
    wide = 2 * width
    step = width + PAD
    planes = fin.shape[0]
    inner = frequency(lax.broadcasted_iota(jnp.int32, (width, wide), 0), width).astype(jnp.float32)
    lane = lax.broadcasted_iota(jnp.int32, (width, wide), 1)
    outer = frequency(lax.rem(lane, width), width).astype(jnp.float32)
    sign = jnp.where(lane < width, 1.0, -1.0)
    for p in range(count):
        slant[p] = par[p, 1:2, :] * inner + par[p, 2:3, :] * outer

    def planes_of(t, who):
        def pair_of(i, carry):
            where, plane = i // (planes // 2), lax.rem(i, planes // 2) * 2
            start = ((t * 2 + where) * 2 + who) * planes + plane
            sums = [None, None]
            for p in range(count):
                pieces = [held[p, pl.ds(pl.multiple_of((start + u) * step, 8), width), :] for u in range(2)]
                plain = jnp.concatenate(pieces, 1)
                turned = jnp.concatenate([pltpu.roll(piece, width, 1) * sign for piece in pieces], 1)
                rhs = jnp.concatenate([plain, turned], 0).astype(jnp.bfloat16)
                value = jnp.dot(table[p], rhs, preferred_element_type=jnp.float32)
                for u in range(2):
                    limit = par[p, 0:1, :] * frequency(start + u, width).astype(jnp.float32)
                    gain = jnp.where(slant[p] + limit <= 0.0, par[p, 3:4, :], 0.0)
                    term = value[:, u * wide : (u + 1) * wide] * gain
                    sums[u] = term if p == 0 else sums[u] + term
            for u in range(2):
                acc[t, where, who, plane + u] = sums[u]
            return carry

        lax.fori_loop(0, planes, pair_of, 0, unroll=True)

    barrier = pltpu.get_barrier_semaphore()
    others = [pair] + [mate(k)[1] for k in range(1, group)] + [far(k)[1] for k in range(1, n_z)]
    for other in others:
        pl.semaphore_signal(barrier, inc=1, device_id=other, device_id_type=MESH)
    planes_of(lax.rem(z + 1, n_z), 1 - core)
    pl.semaphore_wait(barrier, len(others))

    def bands(m):
        return pl.ds(pl.multiple_of(lax.rem(m, n_col) * band, 8), band)

    small1 = send(cls, cgot1, cs1, cr1, pair)
    first = []
    for k in range(n_z):
        t = lax.rem(z + 1 + k, n_z)
        if k:
            planes_of(t, 1 - core)
        first.append(send(acc.at[t, :, 1 - core], got1.at[k], s1.at[k], r1.at[k], pair))
        planes_of(t, core)
    small1.wait()
    csum1[...] = cls[...] + cgot1[...]
    small2 = [send(csum1, cgot2.at[k], cs2.at[k], cr2.at[k], mate(k + 1)[1]) for k in range(group - 1)]
    main = planes - 1
    second, across_z = [], []
    for k in range(n_z):
        t = lax.rem(z + 1 + k, n_z)
        first[k].wait()
        for half in range(2):
            sum1[k, half] = acc[t, half, core] + got1[k, half]
        for g in range(group - 1):
            m, to = mate(g + 1)
            second.append(
                send(
                    sum1.at[k, m // n_col, pl.ds(0, main), bands(m), :], got2.at[k, g], s2.at[k, g], r2.at[k, g], to
                )
            )
        if k < n_z - 1:
            across_z.append(send(sum1.at[k, :, main], zgot.at[k], sz.at[k], rz.at[k], far(k + 1)[1]))
    for copy in small2:
        copy.wait()
    small = csum1[...]
    for k in range(group - 1):
        small = small + cgot2[k]
    csum2[...] = small
    small3 = [send(csum2, cgot3.at[k], cs3.at[k], cr3.at[k], far(k + 1)[1]) for k in range(n_z - 1)]
    third = []
    for k in range(n_z):
        for g in range(group - 1):
            second[k * (group - 1) + g].wait()
        total = sum1[k, x, pl.ds(0, main), bands(member), :]
        for g in range(group - 1):
            total = total + got2[k, g]
        sum2[k] = total
        if k < n_z - 1:
            third.append(send(sum2.at[k], got3.at[k], s3.at[k], r3.at[k], far(k + 1)[1]))
        if k == n_z // 2 - 1:
            for copy in across_z:
                copy.wait()
            for half in range(2):
                total = sum1[n_z - 1, half, main]
                for d in range(n_z - 1):
                    total = total + zgot[d, half]
                zsum[half] = total
            closing = []
            for g in range(group - 1):
                m, to = mate(g + 1)
                closing.append(send(zsum.at[m // n_col, bands(m), :], ygot.at[g], sy.at[g], ry.at[g], to))

    for copy in small3:
        copy.wait()
    small = csum2[...]
    for k in range(n_z - 1):
        small = small + cgot3[k]
    shape = (band, 2 * width)
    middle = frequency(col * band + lax.broadcasted_iota(jnp.int32, shape, 0), width)
    last = frequency(lax.broadcasted_iota(jnp.int32, shape, 1) % width, width)
    factors = []
    for plane in range(planes):
        axes = (jnp.full(shape, 1, jnp.int32) * frequency(row * planes + plane, width), middle, last)
        total = jnp.zeros(shape, jnp.float32)
        for perm in range(6):
            beam, across = 4 * axes[BEAM_LIST[perm]], axes[ACROSS_LIST[perm]]
            for tilt in range(TILTS):
                share = small[0:1, perm * TILTS + tilt : perm * TILTS + tilt + 1]
                total = total + jnp.where(beam <= (5 + 2 * tilt) * across, share, 0.0)
        factors.append(jnp.sqrt(total + wiener_offset))
    for copy in third + closing:
        copy.wait()
    for plane in range(planes):
        if plane < main:
            value = sum2[n_z - 1, plane]
            for k in range(n_z - 1):
                value = value + got3[k, plane]
        else:
            value = zsum[x, bands(member), :]
            for g in range(group - 1):
                value = value + ygot[g]
        fin[plane] = value / factors[plane]


def finish_kernel(width, fin, out):
    planes, band, _ = fin.shape
    half = band // 2
    left = lax.broadcasted_iota(jnp.int32, (half, 2 * width), 1) < width
    for plane in range(planes):
        even = fin[plane, pl.ds(0, half, stride=2), :]
        odd = fin[plane, pl.ds(1, half, stride=2), :]
        real = jnp.where(left, even, pltpu.roll(odd, width, 1))
        imag = jnp.where(left, pltpu.roll(even, width, 1), odd)
        for k in range(half):
            lanes = pl.ds(k * 2 * width, 2 * width)
            out[0, plane : plane + 1, lanes] = real[k : k + 1]
            out[1, plane : plane + 1, lanes] = imag[k : k + 1]


def finish(fin, width):
    planes, band, _ = fin.shape
    vmem = pl.BlockSpec(memory_space=pltpu.VMEM)
    return pl.pallas_call(
        lambda *refs: finish_kernel(width, *refs),
        in_specs=[vmem],
        out_specs=vmem,
        out_shape=jax.ShapeDtypeStruct((2, planes, band * width), jnp.float32),
        compiler_params=pltpu.CompilerParams(vmem_limit_bytes=32 << 20),
        name="finish",
    )(pltpu.with_memory_space_constraint(fin, pltpu.VMEM))


def exchange(held, table, par, cls, n_row, n_col, width):
    n_z = n_row // 4
    planes = width // n_row
    band = width // n_col
    group = 2 * n_col
    wide = 2 * width
    count = held.shape[0]
    operands = [pltpu.with_memory_space_constraint(a, pltpu.VMEM) for a in (held, table, par, cls)]
    vmem = pl.BlockSpec(memory_space=pltpu.VMEM)
    f32 = jnp.float32
    dma = pltpu.SemaphoreType.DMA
    return pl.pallas_call(
        lambda *refs: exchange_kernel(n_z, n_col, width, *refs),
        in_specs=[vmem] * 4,
        out_specs=vmem,
        out_shape=pltpu.VMEM((planes, band, wide), f32),
        scratch_shapes=[
            pltpu.VMEM((n_z, 2, 2, planes, width, wide), f32),
            pltpu.VMEM((count, width, wide), f32),
            pltpu.VMEM((n_z, 2, planes, width, wide), f32),
            pltpu.VMEM((n_z, 2, planes, width, wide), f32),
            pltpu.VMEM((n_z, group - 1, planes - 1, band, wide), f32),
            pltpu.VMEM((n_z, planes - 1, band, wide), f32),
            pltpu.VMEM((n_z - 1, planes - 1, band, wide), f32),
            pltpu.VMEM((n_z - 1, 2, width, wide), f32),
            pltpu.VMEM((2, width, wide), f32),
            pltpu.VMEM((group - 1, band, wide), f32),
            pltpu.VMEM((8, 128), f32),
            pltpu.VMEM((8, 128), f32),
            pltpu.VMEM((group - 1, 8, 128), f32),
            pltpu.VMEM((8, 128), f32),
            pltpu.VMEM((n_z - 1, 8, 128), f32),
            dma((n_z,)), dma((n_z,)), dma((n_z, group - 1)), dma((n_z, group - 1)),
            dma((n_z - 1,)), dma((n_z - 1,)),
            dma, dma, dma((group - 1,)), dma((group - 1,)), dma((n_z - 1,)), dma((n_z - 1,)),
            dma((n_z - 1,)), dma((n_z - 1,)), dma((group - 1,)), dma((group - 1,)),
        ],
        compiler_params=pltpu.CompilerParams(collective_id=0, has_side_effects=True, vmem_limit_bytes=32 << 20),
        name="exchange",
    )(*operands)


def solution(mesh):
    n_row, n_col = mesh.shape["row"], mesh.shape["col"]

    def body(particles, orientation, tilt, weight):
        width = particles.shape[1]
        parts = transform(particles, orientation, tilt, weight)
        return finish(exchange(*parts, n_row, n_col, width), width)

    placed = (P(("row", "col"), None, None), P(("row", "col")), P(("row", "col")), P(("row", "col")))
    return jax.shard_map(body, mesh=mesh, in_specs=placed, out_specs=P(None, "row", "col"), check_vma=False)
```

profile of v0, /device:TPU:0, one launch (start us, length us, event | category | flops | bytes accessed | tf_op | source)
XLA Modules:
  0.0 31.4 jit_solution(14743765233714177065)
XLA Ops:
  0.0 0.0 copy-start
  0.0 1.2 %copy-done = bf16[2,64,4096]{2,1,0:T(8,128)(2,1)S(1)} copy-done((bf16[2,64,4096]{2,1,0:T(8,128)(2,1)S(1)}, bf16[2,64,4096]{2,1,0:T(8,128)(2,1)}, u32[]{:S(2)}) %copy-start) | copy-done | bytes 1048600
  1.2 0.0 copy-start.1
  1.2 0.9 %copy-done.1 = bf16[2,256,256]{2,1,0:T(8,128)(2,1)S(1)} copy-done((bf16[2,256,256]{2,1,0:T(8,128)(2,1)S(1)}, bf16[2,256,256]{2,1,0:T(8,128)(2,1)}, u32[]{:S(2)}) %copy-start.1) | copy-done | bytes 262168
  2.2 0.0 copy-start.2
  2.2 0.9 %copy-done.2 = bf16[2,256,128]{2,1,0:T(8,128)(2,1)S(1)} copy-done((bf16[2,256,128]{2,1,0:T(8,128)(2,1)S(1)}, bf16[2,256,128]{2,1,0:T(8,128)(2,1)}, u32[]{:S(2)}) %copy-start.2) | copy-done | bytes 131096
  3.1 0.0 copy-start.3
  3.1 0.8 %copy-done.3 = bf16[2,128,64]{2,1,0:T(8,128)(2,1)S(1)} copy-done((bf16[2,128,64]{2,1,0:T(8,128)(2,1)S(1)}, bf16[2,128,64]{2,1,0:T(8,128)(2,1)}, u32[]{:S(2)}) %copy-start.3) | copy-done | bytes 32792
  3.9 0.0 copy-start.4
  3.9 0.8 %copy-done.4 = bf16[2,64,128]{2,1,0:T(8,128)(2,1)S(1)} copy-done((bf16[2,64,128]{2,1,0:T(8,128)(2,1)S(1)}, bf16[2,64,128]{2,1,0:T(8,128)(2,1)}, u32[]{:S(2)}) %copy-start.4) | copy-done | bytes 32792
  4.7 0.0 copy-start.5
  4.7 0.7 %copy-done.5 = s32[2]{0:T(128)S(1)} copy-done((s32[2]{0:T(128)S(1)}, s32[2]{0:T(128)}, u32[]{:S(2)}) %copy-start.5) | copy-done | bytes 32
  5.3 0.0 copy-start.6
  5.3 0.7 %copy-done.6 = s32[2]{0:T(128)S(1)} copy-done((s32[2]{0:T(128)S(1)}, s32[2]{0:T(128)}, u32[]{:S(2)}) %copy-start.6) | copy-done | bytes 32
  6.0 0.0 copy-start.7
  6.0 0.7 %copy-done.7 = f32[2]{0:T(128)S(1)} copy-done((f32[2]{0:T(128)S(1)}, f32[2]{0:T(128)}, u32[]{:S(2)}) %copy-start.7) | copy-done | bytes 32
  6.6 2.7 %transform.1 = (f32[2,4608,128]{2,1,0:T(8,128)S(1)}, bf16[2,64,128]{2,1,0:T(8,128)(2,1)S(1)}, f32[2,8,128]{2,1,0:T(8,128)S(1)}, f32[8,128]{1,0:T(8,128)S(1)}) custom-call(s32[2]{0:T(128)S(1)} %copy-done.5, s32[2]{0:T(128)S(1)} %copy-done.6, f32[2]{0:T(128)S(1)} %copy-done.7, bf16[2,64,4096]{2,1,0:T(8,128)(2,1)S(1)} %copy-done, ...), custom_call_target="tpu_custom_call" | custom-call | tf_op jit(solution)/shard_map/transform/pallas_call | solution.py:161
  9.4 21.2 %exchange.1.refs_0_ = f32[4,32,128]{2,1,0:T(8,128)S(1)} custom-call(f32[2,4608,128]{2,1,0:T(8,128)S(1)} %get-tuple-element.9.refs_0_, bf16[2,64,128]{2,1,0:T(8,128)(2,1)S(1)} %get-tuple-element.10.refs_1_, f32[2,8,128]{2,1,0:T(8,128)S(1)} %get-tuple-element.11.refs_2_, f32[8,128]{1,0:T(8,128)S(1)} %get-tuple-element.12.refs_3_), custom_call_target="tpu_custom_call" | custom-call | tf_op jit(solution)/shard_map/exchange/pallas_call | solution.py:378
  30.6 0.7 %finish.1 = f32[2,4,2048]{2,1,0:T(4,128)} custom-call(f32[4,32,128]{2,1,0:T(8,128)S(1)} %exchange.1.refs_0_), custom_call_target="tpu_custom_call" | custom-call | tf_op jit(solution)/shard_map/finish/pallas_call | solution.py:357
Async XLA Ops:
  0.0 1.2 %copy-start = (bf16[2,64,4096]{2,1,0:T(8,128)(2,1)S(1)}, bf16[2,64,4096]{2,1,0:T(8,128)(2,1)}, u32[]{:S(2)}) copy-start(bf16[2,64,4096]{2,1,0:T(8,128)(2,1)} %refs_3_.1) | copy-start | bytes 3145732
  1.2 0.9 %copy-start.1 = (bf16[2,256,256]{2,1,0:T(8,128)(2,1)S(1)}, bf16[2,256,256]{2,1,0:T(8,128)(2,1)}, u32[]{:S(2)}) copy-start(bf16[2,256,256]{2,1,0:T(8,128)(2,1)} %constant.18.refs_6_) | copy-start | bytes 786436
  2.2 0.9 %copy-start.2 = (bf16[2,256,128]{2,1,0:T(8,128)(2,1)S(1)}, bf16[2,256,128]{2,1,0:T(8,128)(2,1)}, u32[]{:S(2)}) copy-start(bf16[2,256,128]{2,1,0:T(8,128)(2,1)} %constant.17.refs_5_) | copy-start | bytes 393220
  3.1 0.8 %copy-start.3 = (bf16[2,128,64]{2,1,0:T(8,128)(2,1)S(1)}, bf16[2,128,64]{2,1,0:T(8,128)(2,1)}, u32[]{:S(2)}) copy-start(bf16[2,128,64]{2,1,0:T(8,128)(2,1)} %constant.16.refs_4_) | copy-start | bytes 98308
  3.9 0.8 %copy-start.4 = (bf16[2,64,128]{2,1,0:T(8,128)(2,1)S(1)}, bf16[2,64,128]{2,1,0:T(8,128)(2,1)}, u32[]{:S(2)}) copy-start(bf16[2,64,128]{2,1,0:T(8,128)(2,1)} %constant.19.refs_7_) | copy-start | bytes 98308
  4.7 0.7 %copy-start.5 = (s32[2]{0:T(128)S(1)}, s32[2]{0:T(128)}, u32[]{:S(2)}) copy-start(s32[2]{0:T(128)} %refs_0_.1) | copy-start | bytes 28
  5.3 0.7 %copy-start.6 = (s32[2]{0:T(128)S(1)}, s32[2]{0:T(128)}, u32[]{:S(2)}) copy-start(s32[2]{0:T(128)} %refs_1_.1) | copy-start | bytes 28
  6.0 0.7 %copy-start.7 = (f32[2]{0:T(128)S(1)}, f32[2]{0:T(128)}, u32[]{:S(2)}) copy-start(f32[2]{0:T(128)} %refs_2_.1) | copy-start | bytes 28
where the time goes:
time: 31.8 us; the launch traced here: 31.4 us
  Pallas kernels  24.7 us (78%)
  local copies, waits for them, and re-layouts  6.64 us (21%)
    pallas_call x1, Pallas kernels, exchange(): pl.pallas_call(lambda *refs: exchange_kernel(n_z, n_col, width, *refs), i...  21.2 us
    unnamed x16, local copies, waits for them, and re-layouts  6.64 us
    pallas_call x1, Pallas kernels, transform(): pl.pallas_call(lambda *refs: transform_kernel(width, *refs), grid=(count,...  2.75 us
    pallas_call x1, Pallas kernels, finish(): pl.pallas_call(lambda *refs: finish_kernel(width, *refs), in_specs=[vmem]...  0.73 us

commit v1 on v0

--- a/solution.py
+++ b/solution.py
@@ -175,7 +175,7 @@
         ],
         compiler_params=pltpu.CompilerParams(vmem_limit_bytes=32 << 20),
         name="transform",
-    )(orientation, tilt, weight, particles, *consts)
+    )(*(pltpu.with_memory_space_constraint(a, pltpu.HBM) for a in (orientation, tilt, weight, particles, *consts)))
 
 
 def exchange_kernel(

time: 31.8 us -> 25.4 us (0.80); the launches traced: 31.4 us -> 25.4 us
  local copies, waits for them, and re-layouts: 6.64 us -> 0 us
  Pallas kernels: 24.7 us -> 25.3 us
    unnamed x16 -> x0, local copies, waits for them, and re-layouts: 6.64 us -> none
    pallas_call x1, Pallas kernels: 2.75 us -> 4.33 us  [transform(): pl.pallas_call(lambda *refs: transform_kernel(width, *refs), grid=(count,...]
    pallas_call x1, Pallas kernels: 21.2 us -> 20.3 us  [exchange(): pl.pallas_call(lambda *refs: exchange_kernel(n_z, n_col, width, *refs), i...]
where the time goes in v1:
time: 25.4 us
  Pallas kernels  25.3 us (100%)
    pallas_call x1, Pallas kernels, exchange(): pl.pallas_call(lambda *refs: exchange_kernel(n_z, n_col, width, *refs), i...  20.3 us
    pallas_call x1, Pallas kernels, transform(): pl.pallas_call(lambda *refs: transform_kernel(width, *refs), grid=(count,...  4.33 us
    pallas_call x1, Pallas kernels, finish(): pl.pallas_call(lambda *refs: finish_kernel(width, *refs), in_specs=[vmem]...  0.73 us

profile of v1, /device:TPU:0, one launch (start us, length us, event | category | flops | bytes accessed | tf_op | source)
XLA Modules:
  0.0 25.4 jit_solution(10401775789797072341)
XLA Ops:
  0.0 4.3 %transform.1 = (f32[2,4608,128]{2,1,0:T(8,128)S(1)}, bf16[2,64,128]{2,1,0:T(8,128)(2,1)S(1)}, f32[2,8,128]{2,1,0:T(8,128)S(1)}, f32[8,128]{1,0:T(8,128)S(1)}) custom-call(s32[2]{0:T(128)} %refs_0_.1, s32[2]{0:T(128)} %refs_1_.1, f32[2]{0:T(128)} %refs_2_.1, bf16[2,64,4096]{2,1,0:T(8,128)(2,1)} %refs_3_.1, bf16[2,128,64]{2,1,0:T(8,128)(2,1)} %constant.16.refs_4_, ...), custom_call_target="tpu_custom_call" | custom-call | tf_op jit(solution)/shard_map/transform/pallas_call | solution.py:161
  4.3 20.3 %exchange.1.refs_0_ = f32[4,32,128]{2,1,0:T(8,128)S(1)} custom-call(f32[2,4608,128]{2,1,0:T(8,128)S(1)} %get-tuple-element.9.refs_0_, bf16[2,64,128]{2,1,0:T(8,128)(2,1)S(1)} %get-tuple-element.10.refs_1_, f32[2,8,128]{2,1,0:T(8,128)S(1)} %get-tuple-element.11.refs_2_, f32[8,128]{1,0:T(8,128)S(1)} %get-tuple-element.12.refs_3_), custom_call_target="tpu_custom_call" | custom-call | tf_op jit(solution)/shard_map/exchange/pallas_call | solution.py:378
  24.6 0.7 %finish.1 = f32[2,4,2048]{2,1,0:T(4,128)} custom-call(f32[4,32,128]{2,1,0:T(8,128)S(1)} %exchange.1.refs_0_), custom_call_target="tpu_custom_call" | custom-call | tf_op jit(solution)/shard_map/finish/pallas_call | solution.py:357
